TPU v7x, 128 devices: a whole 4x4x4 slice. The times are simulated.
128 devices in a mesh: gx: 8 (over z, core), gy: 16 (over y, x).
Axes of the slice: x: 4, y: 4, z: 4, core: 2. Of those that a mesh axis runs over, the one named last changes fastest.
Arguments:
- gradient: float32 [64, 4096], P('gx', 'gy'), may hold values from -6 to 6
- warm_start: float32 [64, 4096], P('gx', 'gy'), may hold values from -3 to 3
- viscosity: float32 [32, 64, 4096], P(None, 'gx', 'gy'), may hold values from 1 to 10
- friction_coef: float32 [64, 4096], P('gx', 'gy'), may hold values from 0.5 to 5
- slide_dir: float32 [2, 64, 4096], P(None, 'gx', 'gy'), may hold values from -4 to 4
- obs_weight: float32 [64, 4096], P('gx', 'gy'), may hold values from 0.5 to 2
- ice_mask: int32 [64, 4096], P('gx', 'gy'), may hold values 0 or 1
- grounded: int32 [64, 4096], P('gx', 'gy'), may hold values 0 or 1
Outputs:
- solution: float32 [64, 4096], P('gx', 'gy')
- residual: float32 [64, 4096], P('gx', 'gy')
All inputs are finite; a program needn't handle non-finite values. No bound on the sum of `ice_mask` or of `grounded` on one device may be relied on, other than what follows from the above.
Results may differ from a plain program's by a relative error of at most 0.00075.
Values sent between devices are 32-bit elements; how exact they have to be, the bound alone decides.
A program may use at most 128 MiB of HBM per device.

v0:
```python
import jax
import jax.numpy as jnp
from jax import lax
from jax.sharding import Mesh
from jax.sharding import PartitionSpec as P

ITERS = 2
GX_GY = ("gx_0", "gx_1", "gy_0", "gy_1")
GX = ("gx_0", "gx_1")
GY = ("gy_0", "gy_1")
vert_coupling = 128.0
sink_rate = 0.0625
bed_drag = 0.5
offset_weight = 0.0019
cross_share = 0.5
reg_gamma = 0.02
reg_smooth = 1.0
diag_scale = 0.003
neighbour_offsets = [
    (step_z, step_x, step_y)
    for step_z in (-1, 0, 1)
    for step_x in (-1, 0, 1)
    for step_y in (-1, 0, 1)
    if step_x != 0 or step_y != 0
]


def by_axis(value, axes):
    for axis in axes:
        value = lax.psum(value, axis)
    return value


def extended(block, sides, width):
    for axis, dim in sides:
        count = lax.axis_size(axis)
        forward = [(i, i + 1) for i in range(count - 1)]
        backward = [(target, source) for source, target in forward]
        low = lax.ppermute(
            lax.slice_in_dim(block, block.shape[dim] - width, None, axis=dim), axis, forward
        )
        high = lax.ppermute(lax.slice_in_dim(block, 0, width, axis=dim), axis, backward)
        block = jnp.concatenate([low, block, high], axis=dim)
    return block


def couple(field_ext, eta_ext):
    levels = eta_ext.shape[0]
    span_x = eta_ext.shape[1] - 2
    span_y = eta_ext.shape[2] - 2
    padded_field = jnp.pad(field_ext, ((0, 0), (1, 1), (0, 0), (0, 0)))
    padded_eta = jnp.pad(eta_ext, ((1, 1), (0, 0), (0, 0)))
    center = eta_ext[:, 1 : 1 + span_x, 1 : 1 + span_y]
    along_one = jnp.zeros((levels, span_x, span_y), jnp.float32)
    along_two = jnp.zeros((levels, span_x, span_y), jnp.float32)
    for step_z, step_x, step_y in neighbour_offsets:
        near_eta = padded_eta[
            1 + step_z : 1 + step_z + levels,
            1 + step_x : 1 + step_x + span_x,
            1 + step_y : 1 + step_y + span_y,
        ]
        weight = (
            offset_weight / (abs(step_x) + abs(step_y) + abs(step_z)) * 0.5 * (center + near_eta)
        )
        near_field = padded_field[
            :,
            1 + step_z : 1 + step_z + levels,
            1 + step_x : 1 + step_x + span_x,
            1 + step_y : 1 + step_y + span_y,
        ]
        along_one = along_one + weight * near_field[0]
        along_two = along_two + weight * near_field[1]
        if step_x != 0 and step_y != 0:
            twist_weight = cross_share * step_x * step_y * weight
            along_one = along_one + twist_weight * near_field[1]
            along_two = along_two + twist_weight * near_field[0]
    return jnp.stack([along_one, along_two])


def tridiagonal(link_weights, diagonal, rhs_cols):
    levels = diagonal.shape[0]
    pivot_value = diagonal[0]
    ratios = [-link_weights[0] / pivot_value]
    partial_value = [rhs_cols[:, 0] / pivot_value]
    for layer_index in range(1, levels):
        pivot_value = diagonal[layer_index] + link_weights[layer_index - 1] * ratios[-1]
        partial_value.append(
            (rhs_cols[:, layer_index] + link_weights[layer_index - 1] * partial_value[-1])
            / pivot_value
        )
        if layer_index < levels - 1:
            ratios.append(-link_weights[layer_index] / pivot_value)
    result = [partial_value[-1]]
    for layer_index in range(levels - 2, -1, -1):
        result.insert(0, partial_value[layer_index] - ratios[layer_index] * result[0])
    return jnp.stack(result, axis=1)


def responses(viscosity, friction):
    levels = viscosity.shape[0]
    link_weights = vert_coupling * 0.5 * (viscosity[:-1] + viscosity[1:])
    zero_layer = jnp.zeros_like(viscosity[:1])
    diagonal = (
        jnp.concatenate([zero_layer, link_weights])
        + jnp.concatenate([link_weights, zero_layer])
        + sink_rate * viscosity
    )
    diagonal = diagonal.at[0].add(bed_drag * friction)
    unit_rhs = jnp.zeros((2,) + viscosity.shape, jnp.float32)
    unit_rhs = unit_rhs.at[0, 0].set(1.0).at[1, levels - 1].set(1.0)
    solved = tridiagonal(link_weights, diagonal, unit_rhs)
    return (solved[0], solved[1])


def regularize(centre_ext):
    middle = centre_ext[1:-1, 1:-1]
    beside_all = (
        centre_ext[2:, 1:-1] + centre_ext[:-2, 1:-1] + centre_ext[1:-1, 2:] + centre_ext[1:-1, :-2]
    )
    return reg_gamma * (middle + reg_smooth * (4.0 * middle - beside_all))


def paired_dots(residual, precond, image_vec):
    return (
        by_axis(jnp.sum(residual * precond), GX_GY),
        by_axis(jnp.sum(precond * image_vec), GX_GY),
    )


def on_device(
    gradient, warm_start, viscosity, friction_coef, slide_dir, obs_weight, ice_mask, grounded
):
    ice_float = ice_mask.astype(jnp.float32)
    ground_float = grounded.astype(jnp.float32)
    friction = ground_float * friction_coef
    source = (ice_float * ground_float * friction_coef)[None] * slide_dir
    obs = ice_float * obs_weight
    inverse_diag = 1.0 / (
        reg_gamma * (1.0 + 4.0 * reg_smooth)
        + diag_scale * ice_float * ground_float * friction_coef * friction_coef
    )
    viscosity_wide = extended(viscosity, ((GX, 1), (GY, 2)), 2)
    columns = jnp.concatenate([source, obs[None], friction[None]], axis=0)
    column_wide = extended(columns, ((GX, 1), (GY, 2)), 2)
    safe_eta = jnp.where(viscosity_wide > 0.0, viscosity_wide, 1.0)
    bottom_wide, top_wide = responses(safe_eta, column_wide[3])
    bottom_inner = bottom_wide[:, 1:-1, 1:-1]
    top_inner = top_wide[:, 1:-1, 1:-1]
    bottom_own = bottom_wide[:, 2:-2, 2:-2]
    top_own = top_wide[:, 2:-2, 2:-2]

    def hessian(direction):
        wide_dir = extended(direction, ((GX, 0), (GY, 1)), 2)
        spread = column_wide[:2] * wide_dir[None]
        first_state = bottom_wide[None] * spread[:, None]
        coupled = couple(first_state, viscosity_wide)
        surface = spread[:, 1:-1, 1:-1] * bottom_inner[-1][None] + jnp.sum(
            top_inner[None] * coupled, axis=1
        )
        traction = column_wide[2, 1:-1, 1:-1][None] * surface
        second_state = top_inner[None] * traction[:, None]
        coupled_back = couple(second_state, viscosity_wide[:, 1:-1, 1:-1])
        basal_part = traction[:, 1:-1, 1:-1] * top_own[0][None] + jnp.sum(
            bottom_own[None] * coupled_back, axis=1
        )
        return jnp.sum(source * basal_part, axis=0) + regularize(wide_dir[1:-1, 1:-1])

    solution = warm_start
    residual = gradient - hessian(warm_start)
    precond = inverse_diag * residual
    image_vec = hessian(precond)
    norm_now, product = paired_dots(residual, precond, image_vec)
    step_size = norm_now / product
    direction = precond
    along_dir = image_vec
    for iteration in range(ITERS):
        solution = solution + step_size * direction
        residual = residual - step_size * along_dir
        if iteration + 1 < ITERS:
            precond = inverse_diag * residual
            image_vec = hessian(precond)
            norm_next, product = paired_dots(residual, precond, image_vec)
            ratio_cg = norm_next / norm_now
            step_size = norm_next / (product - ratio_cg * norm_next / step_size)
            direction = precond + ratio_cg * direction
            along_dir = image_vec + ratio_cg * along_dir
            norm_now = norm_next
    return (solution, residual)


def solution(mesh):
    finer = Mesh(mesh.devices.reshape(4, 2, 4, 4), ("gx_0", "gx_1", "gy_0", "gy_1"))
    return jax.shard_map(
        on_device,
        mesh=finer,
        in_specs=(
            P(GX, GY),
            P(GX, GY),
            P(None, GX, GY),
            P(GX, GY),
            P(None, GX, GY),
            P(GX, GY),
            P(GX, GY),
            P(GX, GY),
        ),
        out_specs=(P(GX, GY), P(GX, GY)),
        check_vma=False,
    )
```

profile of v0, /device:TPU:8, one launch (start us, length us, event | category | flops | bytes accessed | tf_op | source)
XLA Modules:
  0.0 279.2 jit_solution(12042140770638936635)
XLA Ops:
  5.9 4.9 %collective-permute-start = (f32[4,2,256]{2,1,0:T(2,128)S(1)}, f32[4,2,256]{2,1,0:T(2,128)S(1)}, u32[]{:S(2)}, u32[]{:S(2)}) collective-permute-start(f32[4,2,256]{2,1,0:T(2,128)S(1)} %get-tuple-element.246), channel_id=1, source_target_pairs={{0,16},{16,32},{32,48},{48,64},{64,80},{80,96},{96,112},{1,17},{17... | collective-permute-start | bytes 24584 | tf_op jit(solution)/shard_map/ppermute | solution.py:39
  13.2 4.3 %collective-permute-start.8 = (f32[32,2,256]{2,1,0:T(2,128)S(1)}, f32[32,2,256]{2,1,0:T(2,128)S(1)}, u32[]{:S(2)}, u32[]{:S(2)}) collective-permute-start(f32[32,2,256]{2,1,0:T(2,128)S(1)} %get-tuple-element.242), channel_id=1, source_target_pairs={{0,16},{16,32},{32,48},{48,64},{64,80},{80,96},{96,112},{1,17},{17... | collective-permute-start | bytes 196616 | tf_op jit(solution)/shard_map/ppermute | solution.py:39
  23.0 4.6 %collective-permute-start.7 = (f32[12,2]{1,0:T(8,128)S(1)}, f32[12,2]{1,0:T(8,128)S(1)}, u32[]{:S(2)}, u32[]{:S(2)}) collective-permute-start(f32[12,2]{1,0:T(8,128)S(1)} %get-tuple-element.253), channel_id=1, source_target_pairs={{1,0},{2,1},{3,2},{4,3},{5,4},{6,5},{7,6},{8,7},{9,8},{10,9},{11,1... | collective-permute-start | bytes 296 | tf_op jit(solution)/shard_map/ppermute | solution.py:42
  29.6 6.0 %collective-permute-start.3 = (f32[4,12,2]{2,1,0:T(8,128)S(1)}, f32[4,12,2]{2,1,0:T(8,128)S(1)}, u32[]{:S(2)}, u32[]{:S(2)}) collective-permute-start(f32[4,12,2]{2,1,0:T(8,128)S(1)} %get-tuple-element.245), channel_id=1, source_target_pairs={{1,0},{2,1},{3,2},{4,3},{5,4},{6,5},{7,6},{8,7},{9,8},{10,9},{11,1... | collective-permute-start | bytes 1160 | tf_op jit(solution)/shard_map/ppermute | solution.py:42
  41.1 6.3 %collective-permute-start.11 = (f32[32,12,2]{2,1,0:T(8,128)S(1)}, f32[32,12,2]{2,1,0:T(8,128)S(1)}, u32[]{:S(2)}, u32[]{:S(2)}) collective-permute-start(f32[32,12,2]{2,1,0:T(8,128)S(1)} %get-tuple-element.239), channel_id=1, source_target_pairs={{1,0},{2,1},{3,2},{4,3},{5,4},{6,5},{7,6},{8,7},{9,8},{10,9},{11,1... | collective-permute-start | bytes 9224 | tf_op jit(solution)/shard_map/ppermute | solution.py:42
  48.2 4.2 %collective-permute-done.10 = f32[32,12,2]{2,1,0:T(8,128)S(1)} collective-permute-done((f32[32,12,2]{2,1,0:T(8,128)S(1)}, f32[32,12,2]{2,1,0:T(8,128)S(1)}, u32[]{:S(2)}, u32[]{:S(2)}) %collective-permute-start.10) | collective-permute-done | bytes 3104 | tf_op jit(solution)/shard_map/ppermute | solution.py:39
  60.6 9.6 %fusion.241 = (f32[1,32,10,258]{3,2,1,0:T(8,128)}, f32[32,10,258]{2,1,0:T(8,128)S(1)}, f32[32,10,258]{2,1,0:T(8,128)S(1)}, f32[32,10,258]{2,1,0:T(8,128)S(1)}, f...) fusion(f32[2,32,12,260]{3,2,1,0:T(8,128)S(1)} %broadcast_multip, ...), kind=kLoop, calls=%fused_computation.521 | loop fusion | flops 10815360 | bytes 27130368 | tf_op jit(solution)/shard_map/stack | solution.py:77
  70.2 9.7 %fusion.242 = f32[1,32,10,258]{3,2,1,0:T(8,128)} fusion(f32[32,10,258]{2,1,0:T(8,128)} %get-tuple-element.109, f32[32,10,258]{2,1,0:T(8,128)} %get-tuple-element.108, f32[32,10,258]{2,1,0:T(8,128)} %get-tuple-element.107, f32[32,10,258]{2,1,0:T(8,128)} %get-tuple-element.106, f32[32,10,258]{2,1,0:T(8,128)} %get-tuple-element.105, ...), kind=kLoop, calls=%fused_computation.522 | loop fusion | flops 7843200 | bytes 22459392 | tf_op jit(solution)/shard_map/stack | solution.py:77
  83.3 4.4 %fusion.518 = (f32[1,32,8,256]{3,2,1,0:T(8,128)}, f32[32,8,256]{2,1,0:T(8,128)}, f32[32,8,256]{2,1,0:T(8,128)}, f32[32,8,256]{2,1,0:T(8,128)}, f32[32,8,256]{2,1...) fusion(f32[2,32,10,258]{3,2,1,0:T(8,128)S(1)} %broadcast_multip, ...), kind=kLoop, calls=%fused_computation.1103 | loop fusion | flops 8716288 | bytes 13500416 | tf_op jit(solution)/shard_map/stack | solution.py:77
  87.7 4.5 %fusion.515 = f32[1,32,8,256]{3,2,1,0:T(8,128)} fusion(f32[32,8,256]{2,1,0:T(8,128)} %get-tuple-element.84, f32[32,8,256]{2,1,0:T(8,128)} %get-tuple-element.83, f32[32,8,256]{2,1,0:T(8,128)} %get-tuple-element.82, f32[32,8,256]{2,1,0:T(8,128)} %get-tuple-element.81, f32[2,32,10,258]{3,2,1,0:T(8,128)S(1)} %broadcast_multiply_fusion.4, ...), kind=kLoop, calls=%fused_computation.1100 | loop fusion | flops 6619136 | bytes 11141120 | tf_op jit(solution)/shard_map/stack | solution.py:77
  106.6 4.7 %collective-permute-start.15 = (f32[12,2]{1,0:T(8,128)S(1)}, f32[12,2]{1,0:T(8,128)S(1)}, u32[]{:S(2)}, u32[]{:S(2)}) collective-permute-start(f32[12,2]{1,0:T(8,128)S(1)} %get-tuple-element.251), channel_id=1, source_target_pairs={{1,0},{2,1},{3,2},{4,3},{5,4},{6,5},{7,6},{8,7},{9,8},{10,9},{11,1... | collective-permute-start | bytes 296 | tf_op jit(solution)/shard_map/ppermute | solution.py:42
  116.0 8.7 %fusion.244 = f32[1,32,10,258]{3,2,1,0:T(8,128)} fusion(f32[32,10,258]{2,1,0:T(8,128)} %get-tuple-element.109, f32[32,10,258]{2,1,0:T(8,128)} %get-tuple-element.108, f32[32,10,258]{2,1,0:T(8,128)} %get-tuple-element.107, f32[32,10,258]{2,1,0:T(8,128)} %get-tuple-element.106, f32[32,10,258]{2,1,0:T(8,128)} %get-tuple-element.105, ...), kind=kLoop, calls=%fused_computation.524 | loop fusion | flops 7843200 | bytes 22459392 | tf_op jit(solution)/shard_map/stack | solution.py:77
  124.7 8.6 %fusion.243 = f32[1,32,10,258]{3,2,1,0:T(8,128)} fusion(f32[32,10,258]{2,1,0:T(8,128)} %get-tuple-element.109, f32[32,10,258]{2,1,0:T(8,128)} %get-tuple-element.108, f32[32,10,258]{2,1,0:T(8,128)} %get-tuple-element.107, f32[32,10,258]{2,1,0:T(8,128)} %get-tuple-element.106, f32[32,10,258]{2,1,0:T(8,128)} %get-tuple-element.105, ...), kind=kLoop, calls=%fused_computation.523 | loop fusion | flops 7843200 | bytes 22459392 | tf_op jit(solution)/shard_map/stack | solution.py:77
  135.8 4.5 %fusion.516 = f32[1,32,8,256]{3,2,1,0:T(8,128)} fusion(f32[32,8,256]{2,1,0:T(8,128)} %get-tuple-element.84, f32[32,8,256]{2,1,0:T(8,128)} %get-tuple-element.83, f32[32,8,256]{2,1,0:T(8,128)} %get-tuple-element.82, f32[32,8,256]{2,1,0:T(8,128)} %get-tuple-element.81, f32[2,32,10,258]{3,2,1,0:T(8,128)S(1)} %broadcast_multiply_fusion.2, ...), kind=kLoop, calls=%fused_computation.1101 | loop fusion | flops 6619136 | bytes 11141120 | tf_op jit(solution)/shard_map/stack | solution.py:77
  140.3 4.5 %fusion.519 = f32[1,32,8,256]{3,2,1,0:T(8,128)} fusion(f32[32,8,256]{2,1,0:T(8,128)} %get-tuple-element.84, f32[2,32,10,258]{3,2,1,0:T(8,128)S(1)} %broadcast_multiply_fusion.2, f32[32,8,256]{2,1,0:T(8,128)} %get-tuple-element.83, f32[32,8,256]{2,1,0:T(8,128)} %get-tuple-element.82, f32[32,8,256]{2,1,0:T(8,128)} %get-tuple-element.81, ...), kind=kLoop, calls=%fused_computation.1104 | loop fusion | flops 6619136 | bytes 11141120 | tf_op jit(solution)/shard_map/stack | solution.py:77
  149.0 12.6 %all-reduce.15 = (f32[]{:T(128)}, f32[]{:T(128)}) all-reduce(f32[]{:T(128)} %get-tuple-element.41, f32[]{:T(128)} %get-tuple-element.40), channel_id=1, replica_groups=mesh['gx_0'=4,'gx_1'=2,'gy_0'=4,'gy_1'=4] {'gx_0'}, use_global_device_ids=true, to_apply=%region_4.5 | all-reduce | flops 2 | bytes 16 | tf_op jit(solution)/shard_map/psum | solution.py:30
  164.7 9.4 %all-reduce.13 = (f32[]{:T(128)}, f32[]{:T(128)}) all-reduce(f32[]{:T(128)} %get-tuple-element.56, f32[]{:T(128)} %get-tuple-element.57), channel_id=1, replica_groups=mesh['gx_0'=4,'gx_1'=2,'gy_0'=4,'gy_1'=4] {'gy_0'}, use_global_device_ids=true, to_apply=%region_6.7 | all-reduce | flops 2 | bytes 16 | tf_op jit(solution)/shard_map/psum | solution.py:30
  174.1 12.6 %all-reduce.11 = (f32[]{:T(128)}, f32[]{:T(128)}) all-reduce(f32[]{:T(128)} %get-tuple-element.48, f32[]{:T(128)} %get-tuple-element.49), channel_id=1, replica_groups=mesh['gx_0'=4,'gx_1'=2,'gy_0'=4,'gy_1'=4] {'gy_1'}, use_global_device_ids=true, to_apply=%region_7.8 | all-reduce | flops 2 | bytes 16 | tf_op jit(solution)/shard_map/psum | solution.py:30
  195.3 6.3 %collective-permute-start.19 = (f32[12,2]{1,0:T(8,128)S(1)}, f32[12,2]{1,0:T(8,128)S(1)}, u32[]{:S(2)}, u32[]{:S(2)}) collective-permute-start(f32[12,2]{1,0:T(8,128)S(1)} %get-tuple-element.249), channel_id=1, source_target_pairs={{1,0},{2,1},{3,2},{4,3},{5,4},{6,5},{7,6},{8,7},{9,8},{10,9},{11,1... | collective-permute-start | bytes 296 | tf_op jit(solution)/shard_map/ppermute | solution.py:42
  205.5 8.8 %fusion.246 = f32[1,32,10,258]{3,2,1,0:T(8,128)} fusion(f32[32,10,258]{2,1,0:T(8,128)} %get-tuple-element.109, f32[32,10,258]{2,1,0:T(8,128)} %get-tuple-element.108, f32[32,10,258]{2,1,0:T(8,128)} %get-tuple-element.107, f32[32,10,258]{2,1,0:T(8,128)} %get-tuple-element.106, f32[32,10,258]{2,1,0:T(8,128)} %get-tuple-element.105, ...), kind=kLoop, calls=%fused_computation.526 | loop fusion | flops 7843200 | bytes 22003200 | tf_op jit(solution)/shard_map/stack | solution.py:77
  214.3 8.6 %fusion.245 = f32[1,32,10,258]{3,2,1,0:T(8,128)} fusion(f32[32,10,258]{2,1,0:T(8,128)} %get-tuple-element.109, f32[32,10,258]{2,1,0:T(8,128)} %get-tuple-element.108, f32[32,10,258]{2,1,0:T(8,128)} %get-tuple-element.107, f32[32,10,258]{2,1,0:T(8,128)} %get-tuple-element.106, f32[32,10,258]{2,1,0:T(8,128)} %get-tuple-element.105, ...), kind=kLoop, calls=%fused_computation.525 | loop fusion | flops 7843200 | bytes 22459392 | tf_op jit(solution)/shard_map/stack | solution.py:77
  238.0 10.6 %all-reduce.14 = (f32[]{:T(128)}, f32[]{:T(128)}) all-reduce(f32[]{:T(128)} %get-tuple-element.39, f32[]{:T(128)} %get-tuple-element.38), channel_id=1, replica_groups=mesh['gx_0'=4,'gx_1'=2,'gy_0'=4,'gy_1'=4] {'gx_0'}, use_global_device_ids=true, to_apply=%region_17.18 | all-reduce | flops 2 | bytes 16 | tf_op jit(solution)/shard_map/psum | solution.py:30
  251.7 7.9 %all-reduce.12 = (f32[]{:T(128)}, f32[]{:T(128)}) all-reduce(f32[]{:T(128)} %get-tuple-element.54, f32[]{:T(128)} %get-tuple-element.55), channel_id=1, replica_groups=mesh['gx_0'=4,'gx_1'=2,'gy_0'=4,'gy_1'=4] {'gy_0'}, use_global_device_ids=true, to_apply=%region_19.20 | all-reduce | flops 2 | bytes 16 | tf_op jit(solution)/shard_map/psum | solution.py:30
  259.5 13.8 %all-reduce.10 = (f32[]{:T(128)}, f32[]{:T(128)}) all-reduce(f32[]{:T(128)} %get-tuple-element.46, f32[]{:T(128)} %get-tuple-element.47), channel_id=1, replica_groups=mesh['gx_0'=4,'gx_1'=2,'gy_0'=4,'gy_1'=4] {'gy_1'}, use_global_device_ids=true, to_apply=%region_20.21 | all-reduce | flops 2 | bytes 16 | tf_op jit(solution)/shard_map/psum | solution.py:30
  (276 shorter events, 91.2 us)
Async XLA Ops:
  1.4 16.1 %collective-permute-start.4 = (f32[2,256]{1,0:T(2,128)S(1)}, f32[2,256]{1,0:T(2,128)S(1)}, u32[]{:S(2)}, u32[]{:S(2)}) collective-permute-start(f32[2,256]{1,0:T(2,128)S(1)} %get-tuple-element.261), channel_id=1, source_target_pairs={{0,16},{16,32},{32,48},{48,64},{64,80},{80,96},{96,112},{1,17},{17... | collective-permute-start | bytes 6152 | tf_op jit(solution)/shard_map/ppermute | solution.py:39
  3.1 15.7 %collective-permute-start.5 = (f32[2,256]{1,0:T(2,128)S(1)}, f32[2,256]{1,0:T(2,128)S(1)}, u32[]{:S(2)}, u32[]{:S(2)}) collective-permute-start(f32[2,256]{1,0:T(2,128)S(1)} %get-tuple-element.262), channel_id=1, source_target_pairs={{16,0},{32,16},{48,32},{64,48},{80,64},{96,80},{112,96},{17,1},{33... | collective-permute-start | bytes 6152 | tf_op jit(solution)/shard_map/ppermute | solution.py:42
  5.2 88.3 %copy-start.51 = (f32[8,256]{1,0:T(8,128)}, f32[8,256]{1,0:T(8,128)S(1)}, u32[]{:S(2)}) copy-start(f32[8,256]{1,0:T(8,128)S(1)} %get-tuple-element.255) | copy-start | bytes 24580
  5.9 47.6 %copy-start.12 = (f32[32,8,256]{2,1,0:T(8,128)S(1)}, f32[32,8,256]{2,1,0:T(8,128)}, u32[]{:S(2)}) copy-start(f32[32,8,256]{2,1,0:T(8,128)} %param.16) | copy-start | bytes 786436
  5.9 17.1 %collective-permute-start = (f32[4,2,256]{2,1,0:T(2,128)S(1)}, f32[4,2,256]{2,1,0:T(2,128)S(1)}, u32[]{:S(2)}, u32[]{:S(2)}) collective-permute-start(f32[4,2,256]{2,1,0:T(2,128)S(1)} %get-tuple-element.246), channel_id=1, source_target_pairs={{0,16},{16,32},{32,48},{48,64},{64,80},{80,96},{96,112},{1,17},{17... | collective-permute-start | bytes 24584 | tf_op jit(solution)/shard_map/ppermute | solution.py:39
  10.8 16.8 %collective-permute-start.1 = (f32[4,2,256]{2,1,0:T(2,128)S(1)}, f32[4,2,256]{2,1,0:T(2,128)S(1)}, u32[]{:S(2)}, u32[]{:S(2)}) collective-permute-start(f32[4,2,256]{2,1,0:T(2,128)S(1)} %get-tuple-element.247), channel_id=1, source_target_pairs={{16,0},{32,16},{48,32},{64,48},{80,64},{96,80},{112,96},{17,1},{33... | collective-permute-start | bytes 24584 | tf_op jit(solution)/shard_map/ppermute | solution.py:42
  13.2 24.2 %collective-permute-start.8 = (f32[32,2,256]{2,1,0:T(2,128)S(1)}, f32[32,2,256]{2,1,0:T(2,128)S(1)}, u32[]{:S(2)}, u32[]{:S(2)}) collective-permute-start(f32[32,2,256]{2,1,0:T(2,128)S(1)} %get-tuple-element.242), channel_id=1, source_target_pairs={{0,16},{16,32},{32,48},{48,64},{64,80},{80,96},{96,112},{1,17},{17... | collective-permute-start | bytes 196616 | tf_op jit(solution)/shard_map/ppermute | solution.py:39
  17.5 36.6 %copy-start.60 = (f32[2,256]{1,0:T(2,128)}, f32[2,256]{1,0:T(2,128)S(1)}, u32[]{:S(2)}) copy-start(f32[2,256]{1,0:T(2,128)S(1)} %collective-permute-done.4) | copy-start | bytes 6148
  17.5 20.5 %collective-permute-start.9 = (f32[32,2,256]{2,1,0:T(2,128)S(1)}, f32[32,2,256]{2,1,0:T(2,128)S(1)}, u32[]{:S(2)}, u32[]{:S(2)}) collective-permute-start(f32[32,2,256]{2,1,0:T(2,128)S(1)} %get-tuple-element.243), channel_id=1, source_target_pairs={{16,0},{32,16},{48,32},{64,48},{80,64},{96,80},{112,96},{17,1},{33... | collective-permute-start | bytes 196616 | tf_op jit(solution)/shard_map/ppermute | solution.py:42
  19.6 10.0 %collective-permute-start.6 = (f32[12,2]{1,0:T(8,128)S(1)}, f32[12,2]{1,0:T(8,128)S(1)}, u32[]{:S(2)}, u32[]{:S(2)}) collective-permute-start(f32[12,2]{1,0:T(8,128)S(1)} %get-tuple-element.252), channel_id=1, source_target_pairs={{0,1},{1,2},{2,3},{3,4},{4,5},{5,6},{6,7},{7,8},{8,9},{9,10},{10,1... | collective-permute-start | bytes 296 | tf_op jit(solution)/shard_map/ppermute | solution.py:39
  23.0 12.7 %collective-permute-start.7 = (f32[12,2]{1,0:T(8,128)S(1)}, f32[12,2]{1,0:T(8,128)S(1)}, u32[]{:S(2)}, u32[]{:S(2)}) collective-permute-start(f32[12,2]{1,0:T(8,128)S(1)} %get-tuple-element.253), channel_id=1, source_target_pairs={{1,0},{2,1},{3,2},{4,3},{5,4},{6,5},{7,6},{8,7},{9,8},{10,9},{11,1... | collective-permute-start | bytes 296 | tf_op jit(solution)/shard_map/ppermute | solution.py:42
  27.7 8.8 %collective-permute-start.2 = (f32[4,12,2]{2,1,0:T(8,128)S(1)}, f32[4,12,2]{2,1,0:T(8,128)S(1)}, u32[]{:S(2)}, u32[]{:S(2)}) collective-permute-start(f32[4,12,2]{2,1,0:T(8,128)S(1)} %get-tuple-element.244), channel_id=1, source_target_pairs={{0,1},{1,2},{2,3},{3,4},{4,5},{5,6},{6,7},{7,8},{8,9},{9,10},{10,1... | collective-permute-start | bytes 1160 | tf_op jit(solution)/shard_map/ppermute | solution.py:39
  29.6 7.6 %collective-permute-start.3 = (f32[4,12,2]{2,1,0:T(8,128)S(1)}, f32[4,12,2]{2,1,0:T(8,128)S(1)}, u32[]{:S(2)}, u32[]{:S(2)}) collective-permute-start(f32[4,12,2]{2,1,0:T(8,128)S(1)} %get-tuple-element.245), channel_id=1, source_target_pairs={{1,0},{2,1},{3,2},{4,3},{5,4},{6,5},{7,6},{8,7},{9,8},{10,9},{11,1... | collective-permute-start | bytes 1160 | tf_op jit(solution)/shard_map/ppermute | solution.py:42
  39.2 13.2 %collective-permute-start.10 = (f32[32,12,2]{2,1,0:T(8,128)S(1)}, f32[32,12,2]{2,1,0:T(8,128)S(1)}, u32[]{:S(2)}, u32[]{:S(2)}) collective-permute-start(f32[32,12,2]{2,1,0:T(8,128)S(1)} %get-tuple-element.238), channel_id=1, source_target_pairs={{0,1},{1,2},{2,3},{3,4},{4,5},{5,6},{6,7},{7,8},{8,9},{9,10},{10,1... | collective-permute-start | bytes 9224 | tf_op jit(solution)/shard_map/ppermute | solution.py:39
  41.1 12.4 %collective-permute-start.11 = (f32[32,12,2]{2,1,0:T(8,128)S(1)}, f32[32,12,2]{2,1,0:T(8,128)S(1)}, u32[]{:S(2)}, u32[]{:S(2)}) collective-permute-start(f32[32,12,2]{2,1,0:T(8,128)S(1)} %get-tuple-element.239), channel_id=1, source_target_pairs={{1,0},{2,1},{3,2},{4,3},{5,4},{6,5},{7,6},{8,7},{9,8},{10,9},{11,1... | collective-permute-start | bytes 9224 | tf_op jit(solution)/shard_map/ppermute | solution.py:42
  96.1 50.7 %copy-start.50 = (f32[8,256]{1,0:T(8,128)}, f32[8,256]{1,0:T(8,128)S(1)}, u32[]{:S(2)}) copy-start(f32[8,256]{1,0:T(8,128)S(1)} %get-tuple-element.60) | copy-start | bytes 24580
  96.2 2.7 collective-permute-start.12
  97.6 5.1 %collective-permute-start.13 = (f32[2,256]{1,0:T(2,128)S(1)}, f32[2,256]{1,0:T(2,128)S(1)}, u32[]{:S(2)}, u32[]{:S(2)}) collective-permute-start(f32[2,256]{1,0:T(2,128)S(1)} %get-tuple-element.260), channel_id=1, source_target_pairs={{16,0},{32,16},{48,32},{64,48},{80,64},{96,80},{112,96},{17,1},{33... | collective-permute-start | bytes 6152 | tf_op jit(solution)/shard_map/ppermute | solution.py:42
  102.7 8.6 %collective-permute-start.14 = (f32[12,2]{1,0:T(8,128)S(1)}, f32[12,2]{1,0:T(8,128)S(1)}, u32[]{:S(2)}, u32[]{:S(2)}) collective-permute-start(f32[12,2]{1,0:T(8,128)S(1)} %get-tuple-element.250), channel_id=1, source_target_pairs={{0,1},{1,2},{2,3},{3,4},{4,5},{5,6},{6,7},{7,8},{8,9},{9,10},{10,1... | collective-permute-start | bytes 296 | tf_op jit(solution)/shard_map/ppermute | solution.py:39
  106.6 6.1 %collective-permute-start.15 = (f32[12,2]{1,0:T(8,128)S(1)}, f32[12,2]{1,0:T(8,128)S(1)}, u32[]{:S(2)}, u32[]{:S(2)}) collective-permute-start(f32[12,2]{1,0:T(8,128)S(1)} %get-tuple-element.251), channel_id=1, source_target_pairs={{1,0},{2,1},{3,2},{4,3},{5,4},{6,5},{7,6},{8,7},{9,8},{10,9},{11,1... | collective-permute-start | bytes 296 | tf_op jit(solution)/shard_map/ppermute | solution.py:42
  188.9 2.6 collective-permute-start.16
  190.2 3.1 %collective-permute-start.17 = (f32[2,256]{1,0:T(2,128)S(1)}, f32[2,256]{1,0:T(2,128)S(1)}, u32[]{:S(2)}, u32[]{:S(2)}) collective-permute-start(f32[2,256]{1,0:T(2,128)S(1)} %get-tuple-element.258), channel_id=1, source_target_pairs={{16,0},{32,16},{48,32},{64,48},{80,64},{96,80},{112,96},{17,1},{33... | collective-permute-start | bytes 6152 | tf_op jit(solution)/shard_map/ppermute | solution.py:42
  193.4 8.2 %collective-permute-start.18 = (f32[12,2]{1,0:T(8,128)S(1)}, f32[12,2]{1,0:T(8,128)S(1)}, u32[]{:S(2)}, u32[]{:S(2)}) collective-permute-start(f32[12,2]{1,0:T(8,128)S(1)} %get-tuple-element.248), channel_id=1, source_target_pairs={{0,1},{1,2},{2,3},{3,4},{4,5},{5,6},{6,7},{7,8},{8,9},{9,10},{10,1... | collective-permute-start | bytes 296 | tf_op jit(solution)/shard_map/ppermute | solution.py:39
  195.3 7.4 %collective-permute-start.19 = (f32[12,2]{1,0:T(8,128)S(1)}, f32[12,2]{1,0:T(8,128)S(1)}, u32[]{:S(2)}, u32[]{:S(2)}) collective-permute-start(f32[12,2]{1,0:T(8,128)S(1)} %get-tuple-element.249), channel_id=1, source_target_pairs={{1,0},{2,1},{3,2},{4,3},{5,4},{6,5},{7,6},{8,7},{9,8},{10,9},{11,1... | collective-permute-start | bytes 296 | tf_op jit(solution)/shard_map/ppermute | solution.py:42
  (62 other events, 457.8 us)
where the time goes:
time: 281 us; the launch traced here: 279 us
  other arithmetic  111 us (40%)
  blocking collectives  73 us (26%)
  starting transfers between devices  60.9 us (22%)
  waiting for transfers between devices  14.1 us (5%)
  local copies, waits for them, and re-layouts  12.1 us (4%)
  between operations  7.96 us (3%)
    another operation x12, other arithmetic, couple(): return jnp.stack([along_one, along_two])  80.1 us
    psum x8, blocking collectives, by_axis(): value = lax.psum(value, axis)  73 us
    ppermute x10, starting transfers between devices, extended(): lax.ppermute(lax.slice_in_dim(block, 0, width, axis=dim), axis, backward)  34.3 us
    ppermute x10, starting transfers between devices, extended(): lax.ppermute(lax.slice_in_dim(block, block.shape[dim] - width, None, axis...  26.6 us
    ppermute x10, waiting for transfers between devices, extended(): lax.ppermute(lax.slice_in_dim(block, 0, width, axis=dim), axis, backward)  9.88 us
    unnamed x147, local copies, waits for them, and re-layouts  6.45 us
  transfers between devices with their start and end apart: 20, of which 7 were waited for; matrix products, arithmetic and copies ran while one was open for 2% of the time, Pallas kernels for 0%

commit v1 on v0

--- a/solution.py
+++ b/solution.py
@@ -27,7 +27,11 @@
 
 def by_axis(value, axes):
     for axis in axes:
-        value = lax.psum(value, axis)
+
+        def store_hubs(shard_in):
+            return jax.lax.all_gather(shard_in, axis_name=axis).sum(axis=0)
+
+        value = store_hubs(value)
     return value
 
 

time: 281 us -> 335 us (1.19)
  local copies, waits for them, and re-layouts: 12.1 us -> 52.8 us
  other arithmetic: 111 us -> 127 us
    psum x8 -> x0, blocking collectives: 73 us -> none  [by_axis(): value = lax.psum(value, axis)]
    unnamed x0 -> x8, blocking collectives: none -> 70.4 us
    unnamed x147 -> x183, local copies, waits for them, and re-layouts: 6.45 us -> 46.6 us
    reduce_sum x0 -> x16, other arithmetic: none -> 14.7 us  [store_hubs(): return jax.lax.all_gather(shard_in, axis_name=axis).sum(axis=0)]
where the time goes in v1:
time: 335 us; the launch traced here: 332 us
  other arithmetic  127 us (38%)
  blocking collectives  70.4 us (21%)
  starting transfers between devices  61.5 us (18%)
  local copies, waits for them, and re-layouts  52.8 us (16%)
  waiting for transfers between devices  12.4 us (4%)
  between operations  8.17 us (2%)
    another operation x12, other arithmetic, couple(): return jnp.stack([along_one, along_two])  80.2 us
    unnamed x8, blocking collectives  70.4 us
    unnamed x183, local copies, waits for them, and re-layouts  46.6 us
    ppermute x10, starting transfers between devices, extended(): lax.ppermute(lax.slice_in_dim(block, 0, width, axis=dim), axis, backward)  34.3 us
    ppermute x10, starting transfers between devices, extended(): lax.ppermute(lax.slice_in_dim(block, block.shape[dim] - width, None, axis...  27.2 us
    reduce_sum x16, other arithmetic, store_hubs(): return jax.lax.all_gather(shard_in, axis_name=axis).sum(axis=0)  14.7 us
    ppermute x10, waiting for transfers between devices, extended(): lax.ppermute(lax.slice_in_dim(block, 0, width, axis=dim), axis, backward)  8.15 us
  transfers between devices with their start and end apart: 20, of which 7 were waited for; matrix products, arithmetic and copies ran while one was open for 2% of the time, Pallas kernels for 0%

profile of v1, /device:TPU:8, one launch (start us, length us, event | category | flops | bytes accessed | tf_op | source)
XLA Modules:
  0.0 332.4 jit_solution(7826285369001129612)
XLA Ops:
  5.9 4.9 %collective-permute-start = (f32[4,2,256]{2,1,0:T(2,128)S(1)}, f32[4,2,256]{2,1,0:T(2,128)S(1)}, u32[]{:S(2)}, u32[]{:S(2)}) collective-permute-start(f32[4,2,256]{2,1,0:T(2,128)S(1)} %get-tuple-element.246), channel_id=1, source_target_pairs={{0,16},{16,32},{32,48},{48,64},{64,80},{80,96},{96,112},{1,17},{17... | collective-permute-start | bytes 24584 | tf_op jit(solution)/shard_map/ppermute | solution.py:43
  13.2 4.3 %collective-permute-start.8 = (f32[32,2,256]{2,1,0:T(2,128)S(1)}, f32[32,2,256]{2,1,0:T(2,128)S(1)}, u32[]{:S(2)}, u32[]{:S(2)}) collective-permute-start(f32[32,2,256]{2,1,0:T(2,128)S(1)} %get-tuple-element.242), channel_id=1, source_target_pairs={{0,16},{16,32},{32,48},{48,64},{64,80},{80,96},{96,112},{1,17},{17... | collective-permute-start | bytes 196616 | tf_op jit(solution)/shard_map/ppermute | solution.py:43
  23.0 4.6 %collective-permute-start.7 = (f32[12,2]{1,0:T(8,128)S(1)}, f32[12,2]{1,0:T(8,128)S(1)}, u32[]{:S(2)}, u32[]{:S(2)}) collective-permute-start(f32[12,2]{1,0:T(8,128)S(1)} %get-tuple-element.253), channel_id=1, source_target_pairs={{1,0},{2,1},{3,2},{4,3},{5,4},{6,5},{7,6},{8,7},{9,8},{10,9},{11,1... | collective-permute-start | bytes 296 | tf_op jit(solution)/shard_map/ppermute | solution.py:46
  29.6 6.0 %collective-permute-start.3 = (f32[4,12,2]{2,1,0:T(8,128)S(1)}, f32[4,12,2]{2,1,0:T(8,128)S(1)}, u32[]{:S(2)}, u32[]{:S(2)}) collective-permute-start(f32[4,12,2]{2,1,0:T(8,128)S(1)} %get-tuple-element.245), channel_id=1, source_target_pairs={{1,0},{2,1},{3,2},{4,3},{5,4},{6,5},{7,6},{8,7},{9,8},{10,9},{11,1... | collective-permute-start | bytes 1160 | tf_op jit(solution)/shard_map/ppermute | solution.py:46
  41.1 6.3 %collective-permute-start.11 = (f32[32,12,2]{2,1,0:T(8,128)S(1)}, f32[32,12,2]{2,1,0:T(8,128)S(1)}, u32[]{:S(2)}, u32[]{:S(2)}) collective-permute-start(f32[32,12,2]{2,1,0:T(8,128)S(1)} %get-tuple-element.239), channel_id=1, source_target_pairs={{1,0},{2,1},{3,2},{4,3},{5,4},{6,5},{7,6},{8,7},{9,8},{10,9},{11,1... | collective-permute-start | bytes 9224 | tf_op jit(solution)/shard_map/ppermute | solution.py:46
  48.1 4.2 %collective-permute-done.10 = f32[32,12,2]{2,1,0:T(8,128)S(1)} collective-permute-done((f32[32,12,2]{2,1,0:T(8,128)S(1)}, f32[32,12,2]{2,1,0:T(8,128)S(1)}, u32[]{:S(2)}, u32[]{:S(2)}) %collective-permute-start.10) | collective-permute-done | bytes 3104 | tf_op jit(solution)/shard_map/ppermute | solution.py:43
  60.6 9.6 %fusion.241 = (f32[1,32,10,258]{3,2,1,0:T(8,128)}, f32[32,10,258]{2,1,0:T(8,128)S(1)}, f32[32,10,258]{2,1,0:T(8,128)S(1)}, f32[32,10,258]{2,1,0:T(8,128)S(1)}, f...) fusion(f32[2,32,12,260]{3,2,1,0:T(8,128)S(1)} %broadcast_multip, ...), kind=kLoop, calls=%fused_computation.521 | loop fusion | flops 10815360 | bytes 27130368 | tf_op jit(solution)/shard_map/stack | solution.py:81
  70.3 9.7 %fusion.242 = f32[1,32,10,258]{3,2,1,0:T(8,128)} fusion(f32[32,10,258]{2,1,0:T(8,128)} %get-tuple-element.109, f32[32,10,258]{2,1,0:T(8,128)} %get-tuple-element.108, f32[32,10,258]{2,1,0:T(8,128)} %get-tuple-element.107, f32[32,10,258]{2,1,0:T(8,128)} %get-tuple-element.106, f32[32,10,258]{2,1,0:T(8,128)} %get-tuple-element.105, ...), kind=kLoop, calls=%fused_computation.522 | loop fusion | flops 7843200 | bytes 22459392 | tf_op jit(solution)/shard_map/stack | solution.py:81
  83.3 4.4 %fusion.518 = (f32[1,32,8,256]{3,2,1,0:T(8,128)}, f32[32,8,256]{2,1,0:T(8,128)}, f32[32,8,256]{2,1,0:T(8,128)}, f32[32,8,256]{2,1,0:T(8,128)}, f32[32,8,256]{2,1...) fusion(f32[2,32,10,258]{3,2,1,0:T(8,128)S(1)} %broadcast_multip, ...), kind=kLoop, calls=%fused_computation.1103 | loop fusion | flops 8716288 | bytes 13500416 | tf_op jit(solution)/shard_map/stack | solution.py:81
  87.7 4.5 %fusion.515 = f32[1,32,8,256]{3,2,1,0:T(8,128)} fusion(f32[32,8,256]{2,1,0:T(8,128)} %get-tuple-element.84, f32[32,8,256]{2,1,0:T(8,128)} %get-tuple-element.83, f32[32,8,256]{2,1,0:T(8,128)} %get-tuple-element.82, f32[32,8,256]{2,1,0:T(8,128)} %get-tuple-element.81, f32[2,32,10,258]{3,2,1,0:T(8,128)S(1)} %broadcast_multiply_fusion.4, ...), kind=kLoop, calls=%fused_computation.1100 | loop fusion | flops 6619136 | bytes 11141120 | tf_op jit(solution)/shard_map/stack | solution.py:81
  108.6 4.7 %collective-permute-start.15 = (f32[12,2]{1,0:T(8,128)S(1)}, f32[12,2]{1,0:T(8,128)S(1)}, u32[]{:S(2)}, u32[]{:S(2)}) collective-permute-start(f32[12,2]{1,0:T(8,128)S(1)} %get-tuple-element.251), channel_id=1, source_target_pairs={{1,0},{2,1},{3,2},{4,3},{5,4},{6,5},{7,6},{8,7},{9,8},{10,9},{11,1... | collective-permute-start | bytes 296 | tf_op jit(solution)/shard_map/ppermute | solution.py:46
  118.2 8.8 %fusion.244 = f32[1,32,10,258]{3,2,1,0:T(8,128)} fusion(f32[32,10,258]{2,1,0:T(8,128)} %get-tuple-element.109, f32[32,10,258]{2,1,0:T(8,128)} %get-tuple-element.108, f32[32,10,258]{2,1,0:T(8,128)} %get-tuple-element.107, f32[32,10,258]{2,1,0:T(8,128)} %get-tuple-element.106, f32[32,10,258]{2,1,0:T(8,128)} %get-tuple-element.105, ...), kind=kLoop, calls=%fused_computation.524 | loop fusion | flops 7843200 | bytes 22003200 | tf_op jit(solution)/shard_map/stack | solution.py:81
  127.0 8.6 %fusion.243 = f32[1,32,10,258]{3,2,1,0:T(8,128)} fusion(f32[32,10,258]{2,1,0:T(8,128)} %get-tuple-element.109, f32[32,10,258]{2,1,0:T(8,128)} %get-tuple-element.108, f32[32,10,258]{2,1,0:T(8,128)} %get-tuple-element.107, f32[32,10,258]{2,1,0:T(8,128)} %get-tuple-element.106, f32[32,10,258]{2,1,0:T(8,128)} %get-tuple-element.105, ...), kind=kLoop, calls=%fused_computation.523 | loop fusion | flops 7843200 | bytes 22459392 | tf_op jit(solution)/shard_map/stack | solution.py:81
  138.1 4.5 %fusion.516 = f32[1,32,8,256]{3,2,1,0:T(8,128)} fusion(f32[32,8,256]{2,1,0:T(8,128)} %get-tuple-element.84, f32[32,8,256]{2,1,0:T(8,128)} %get-tuple-element.83, f32[32,8,256]{2,1,0:T(8,128)} %get-tuple-element.82, f32[32,8,256]{2,1,0:T(8,128)} %get-tuple-element.81, f32[2,32,10,258]{3,2,1,0:T(8,128)S(1)} %broadcast_multiply_fusion.2, ...), kind=kLoop, calls=%fused_computation.1101 | loop fusion | flops 6619136 | bytes 11141120 | tf_op jit(solution)/shard_map/stack | solution.py:81
  142.6 4.5 %fusion.519 = f32[1,32,8,256]{3,2,1,0:T(8,128)} fusion(f32[32,8,256]{2,1,0:T(8,128)} %get-tuple-element.84, f32[2,32,10,258]{3,2,1,0:T(8,128)S(1)} %broadcast_multiply_fusion.2, f32[32,8,256]{2,1,0:T(8,128)} %get-tuple-element.83, f32[32,8,256]{2,1,0:T(8,128)} %get-tuple-element.82, f32[32,8,256]{2,1,0:T(8,128)} %get-tuple-element.81, ...), kind=kLoop, calls=%fused_computation.1104 | loop fusion | flops 6619136 | bytes 11141120 | tf_op jit(solution)/shard_map/stack | solution.py:81
  158.7 12.5 %all-reduce.31 = (f32[4]{0:T(128)}, f32[4]{0:T(128)}) all-reduce(f32[4]{0:T(128)} %dynamic-update-slice.9, f32[4]{0:T(128)} %dynamic-update-slice.13), channel_id=1, replica_groups=mesh['gx_0'=4,'gx_1'=2,'gy_0'=4,'gy_1'=4] {'gx_0'}, use_global_device_ids=true, to_apply=%add.10 | all-reduce | flops 8 | bytes 64
  193.7 9.3 %all-reduce.29 = (f32[4]{0:T(128)}, f32[4]{0:T(128)}) all-reduce(f32[4]{0:T(128)} %dynamic-update-slice.11, f32[4]{0:T(128)} %dynamic-update-slice.15), channel_id=1, replica_groups=mesh['gx_0'=4,'gx_1'=2,'gy_0'=4,'gy_1'=4] {'gy_0'}, use_global_device_ids=true, to_apply=%add.12 | all-reduce | flops 8 | bytes 64
  211.4 12.6 %all-reduce.27 = (f32[4]{0:T(128)}, f32[4]{0:T(128)}) all-reduce(f32[4]{0:T(128)} %dynamic-update-slice.12, f32[4]{0:T(128)} %dynamic-update-slice.16), channel_id=1, replica_groups=mesh['gx_0'=4,'gx_1'=2,'gy_0'=4,'gy_1'=4] {'gy_1'}, use_global_device_ids=true, to_apply=%add.13 | all-reduce | flops 8 | bytes 64
  235.3 6.3 %collective-permute-start.19 = (f32[12,2]{1,0:T(8,128)S(1)}, f32[12,2]{1,0:T(8,128)S(1)}, u32[]{:S(2)}, u32[]{:S(2)}) collective-permute-start(f32[12,2]{1,0:T(8,128)S(1)} %get-tuple-element.249), channel_id=1, source_target_pairs={{1,0},{2,1},{3,2},{4,3},{5,4},{6,5},{7,6},{8,7},{9,8},{10,9},{11,1... | collective-permute-start | bytes 296 | tf_op jit(solution)/shard_map/ppermute | solution.py:46
  245.5 8.8 %fusion.246 = f32[1,32,10,258]{3,2,1,0:T(8,128)} fusion(f32[32,10,258]{2,1,0:T(8,128)} %get-tuple-element.109, f32[32,10,258]{2,1,0:T(8,128)} %get-tuple-element.108, f32[32,10,258]{2,1,0:T(8,128)} %get-tuple-element.107, f32[32,10,258]{2,1,0:T(8,128)} %get-tuple-element.106, f32[32,10,258]{2,1,0:T(8,128)} %get-tuple-element.105, ...), kind=kLoop, calls=%fused_computation.526 | loop fusion | flops 7843200 | bytes 22003200 | tf_op jit(solution)/shard_map/stack | solution.py:81
  254.3 8.6 %fusion.245 = f32[1,32,10,258]{3,2,1,0:T(8,128)} fusion(f32[32,10,258]{2,1,0:T(8,128)} %get-tuple-element.109, f32[32,10,258]{2,1,0:T(8,128)} %get-tuple-element.108, f32[32,10,258]{2,1,0:T(8,128)} %get-tuple-element.107, f32[32,10,258]{2,1,0:T(8,128)} %get-tuple-element.106, f32[32,10,258]{2,1,0:T(8,128)} %get-tuple-element.105, ...), kind=kLoop, calls=%fused_computation.525 | loop fusion | flops 7843200 | bytes 22459392 | tf_op jit(solution)/shard_map/stack | solution.py:81
  280.8 10.0 %all-reduce.30 = (f32[4]{0:T(128)S(1)}, f32[4]{0:T(128)S(1)}) all-reduce(f32[4]{0:T(128)S(1)} %dynamic-update-slice.17, f32[4]{0:T(128)S(1)} %dynamic-update-slice.21), channel_id=1, replica_groups=mesh['gx_0'=4,'gx_1'=2,'gy_0'=4,'gy_1'=4] {'gx_0'}, use_global_device_ids=true, to_apply=%add.18 | all-reduce | flops 8 | bytes 64
  301.1 7.2 %all-reduce.28 = (f32[4]{0:T(128)S(1)}, f32[4]{0:T(128)S(1)}) all-reduce(f32[4]{0:T(128)S(1)} %dynamic-update-slice.19, f32[4]{0:T(128)S(1)} %dynamic-update-slice.23), channel_id=1, replica_groups=mesh['gx_0'=4,'gx_1'=2,'gy_0'=4,'gy_1'=4] {'gy_0'}, use_global_device_ids=true, to_apply=%add.20 | all-reduce | flops 8 | bytes 64
  312.2 13.1 %all-reduce.26 = (f32[4]{0:T(128)S(1)}, f32[4]{0:T(128)S(1)}) all-reduce(f32[4]{0:T(128)S(1)} %dynamic-update-slice.20, f32[4]{0:T(128)S(1)} %dynamic-update-slice.24), channel_id=1, replica_groups=mesh['gx_0'=4,'gx_1'=2,'gy_0'=4,'gy_1'=4] {'gy_1'}, use_global_device_ids=true, to_apply=%add.21 | all-reduce | flops 8 | bytes 64
  (328 shorter events, 146.2 us)
Async XLA Ops:
  1.4 16.1 %collective-permute-start.4 = (f32[2,256]{1,0:T(2,128)S(1)}, f32[2,256]{1,0:T(2,128)S(1)}, u32[]{:S(2)}, u32[]{:S(2)}) collective-permute-start(f32[2,256]{1,0:T(2,128)S(1)} %get-tuple-element.261), channel_id=1, source_target_pairs={{0,16},{16,32},{32,48},{48,64},{64,80},{80,96},{96,112},{1,17},{17... | collective-permute-start | bytes 6152 | tf_op jit(solution)/shard_map/ppermute | solution.py:43
  3.1 15.7 %collective-permute-start.5 = (f32[2,256]{1,0:T(2,128)S(1)}, f32[2,256]{1,0:T(2,128)S(1)}, u32[]{:S(2)}, u32[]{:S(2)}) collective-permute-start(f32[2,256]{1,0:T(2,128)S(1)} %get-tuple-element.262), channel_id=1, source_target_pairs={{16,0},{32,16},{48,32},{64,48},{80,64},{96,80},{112,96},{17,1},{33... | collective-permute-start | bytes 6152 | tf_op jit(solution)/shard_map/ppermute | solution.py:46
  5.2 88.2 %copy-start.52 = (f32[8,256]{1,0:T(8,128)}, f32[8,256]{1,0:T(8,128)S(1)}, u32[]{:S(2)}) copy-start(f32[8,256]{1,0:T(8,128)S(1)} %get-tuple-element.255) | copy-start | bytes 24580
  5.9 47.6 %copy-start.12 = (f32[32,8,256]{2,1,0:T(8,128)S(1)}, f32[32,8,256]{2,1,0:T(8,128)}, u32[]{:S(2)}) copy-start(f32[32,8,256]{2,1,0:T(8,128)} %param.16) | copy-start | bytes 786436
  5.9 17.1 %collective-permute-start = (f32[4,2,256]{2,1,0:T(2,128)S(1)}, f32[4,2,256]{2,1,0:T(2,128)S(1)}, u32[]{:S(2)}, u32[]{:S(2)}) collective-permute-start(f32[4,2,256]{2,1,0:T(2,128)S(1)} %get-tuple-element.246), channel_id=1, source_target_pairs={{0,16},{16,32},{32,48},{48,64},{64,80},{80,96},{96,112},{1,17},{17... | collective-permute-start | bytes 24584 | tf_op jit(solution)/shard_map/ppermute | solution.py:43
  10.8 16.8 %collective-permute-start.1 = (f32[4,2,256]{2,1,0:T(2,128)S(1)}, f32[4,2,256]{2,1,0:T(2,128)S(1)}, u32[]{:S(2)}, u32[]{:S(2)}) collective-permute-start(f32[4,2,256]{2,1,0:T(2,128)S(1)} %get-tuple-element.247), channel_id=1, source_target_pairs={{16,0},{32,16},{48,32},{64,48},{80,64},{96,80},{112,96},{17,1},{33... | collective-permute-start | bytes 24584 | tf_op jit(solution)/shard_map/ppermute | solution.py:46
  13.2 24.2 %collective-permute-start.8 = (f32[32,2,256]{2,1,0:T(2,128)S(1)}, f32[32,2,256]{2,1,0:T(2,128)S(1)}, u32[]{:S(2)}, u32[]{:S(2)}) collective-permute-start(f32[32,2,256]{2,1,0:T(2,128)S(1)} %get-tuple-element.242), channel_id=1, source_target_pairs={{0,16},{16,32},{32,48},{48,64},{64,80},{80,96},{96,112},{1,17},{17... | collective-permute-start | bytes 196616 | tf_op jit(solution)/shard_map/ppermute | solution.py:43
  17.5 36.6 %copy-start.61 = (f32[2,256]{1,0:T(2,128)}, f32[2,256]{1,0:T(2,128)S(1)}, u32[]{:S(2)}) copy-start(f32[2,256]{1,0:T(2,128)S(1)} %collective-permute-done.4) | copy-start | bytes 6148
  17.5 20.5 %collective-permute-start.9 = (f32[32,2,256]{2,1,0:T(2,128)S(1)}, f32[32,2,256]{2,1,0:T(2,128)S(1)}, u32[]{:S(2)}, u32[]{:S(2)}) collective-permute-start(f32[32,2,256]{2,1,0:T(2,128)S(1)} %get-tuple-element.243), channel_id=1, source_target_pairs={{16,0},{32,16},{48,32},{64,48},{80,64},{96,80},{112,96},{17,1},{33... | collective-permute-start | bytes 196616 | tf_op jit(solution)/shard_map/ppermute | solution.py:46
  18.8 35.3 %copy-start.63 = (f32[2,256]{1,0:T(2,128)}, f32[2,256]{1,0:T(2,128)S(1)}, u32[]{:S(2)}) copy-start(f32[2,256]{1,0:T(2,128)S(1)} %collective-permute-done.5) | copy-start | bytes 6148
  19.6 10.0 %collective-permute-start.6 = (f32[12,2]{1,0:T(8,128)S(1)}, f32[12,2]{1,0:T(8,128)S(1)}, u32[]{:S(2)}, u32[]{:S(2)}) collective-permute-start(f32[12,2]{1,0:T(8,128)S(1)} %get-tuple-element.252), channel_id=1, source_target_pairs={{0,1},{1,2},{2,3},{3,4},{4,5},{5,6},{6,7},{7,8},{8,9},{9,10},{10,1... | collective-permute-start | bytes 296 | tf_op jit(solution)/shard_map/ppermute | solution.py:43
  23.0 12.7 %collective-permute-start.7 = (f32[12,2]{1,0:T(8,128)S(1)}, f32[12,2]{1,0:T(8,128)S(1)}, u32[]{:S(2)}, u32[]{:S(2)}) collective-permute-start(f32[12,2]{1,0:T(8,128)S(1)} %get-tuple-element.253), channel_id=1, source_target_pairs={{1,0},{2,1},{3,2},{4,3},{5,4},{6,5},{7,6},{8,7},{9,8},{10,9},{11,1... | collective-permute-start | bytes 296 | tf_op jit(solution)/shard_map/ppermute | solution.py:46
  27.7 8.8 %collective-permute-start.2 = (f32[4,12,2]{2,1,0:T(8,128)S(1)}, f32[4,12,2]{2,1,0:T(8,128)S(1)}, u32[]{:S(2)}, u32[]{:S(2)}) collective-permute-start(f32[4,12,2]{2,1,0:T(8,128)S(1)} %get-tuple-element.244), channel_id=1, source_target_pairs={{0,1},{1,2},{2,3},{3,4},{4,5},{5,6},{6,7},{7,8},{8,9},{9,10},{10,1... | collective-permute-start | bytes 1160 | tf_op jit(solution)/shard_map/ppermute | solution.py:43
  29.6 7.6 %collective-permute-start.3 = (f32[4,12,2]{2,1,0:T(8,128)S(1)}, f32[4,12,2]{2,1,0:T(8,128)S(1)}, u32[]{:S(2)}, u32[]{:S(2)}) collective-permute-start(f32[4,12,2]{2,1,0:T(8,128)S(1)} %get-tuple-element.245), channel_id=1, source_target_pairs={{1,0},{2,1},{3,2},{4,3},{5,4},{6,5},{7,6},{8,7},{9,8},{10,9},{11,1... | collective-permute-start | bytes 1160 | tf_op jit(solution)/shard_map/ppermute | solution.py:46
  39.2 13.2 %collective-permute-start.10 = (f32[32,12,2]{2,1,0:T(8,128)S(1)}, f32[32,12,2]{2,1,0:T(8,128)S(1)}, u32[]{:S(2)}, u32[]{:S(2)}) collective-permute-start(f32[32,12,2]{2,1,0:T(8,128)S(1)} %get-tuple-element.238), channel_id=1, source_target_pairs={{0,1},{1,2},{2,3},{3,4},{4,5},{5,6},{6,7},{7,8},{8,9},{9,10},{10,1... | collective-permute-start | bytes 9224 | tf_op jit(solution)/shard_map/ppermute | solution.py:43
  41.1 12.4 %collective-permute-start.11 = (f32[32,12,2]{2,1,0:T(8,128)S(1)}, f32[32,12,2]{2,1,0:T(8,128)S(1)}, u32[]{:S(2)}, u32[]{:S(2)}) collective-permute-start(f32[32,12,2]{2,1,0:T(8,128)S(1)} %get-tuple-element.239), channel_id=1, source_target_pairs={{1,0},{2,1},{3,2},{4,3},{5,4},{6,5},{7,6},{8,7},{9,8},{10,9},{11,1... | collective-permute-start | bytes 9224 | tf_op jit(solution)/shard_map/ppermute | solution.py:46
  97.1 4.8 %collective-permute-start.12 = (f32[2,256]{1,0:T(2,128)}, f32[2,256]{1,0:T(2,128)}, u32[]{:S(2)}, u32[]{:S(2)}) collective-permute-start(f32[2,256]{1,0:T(2,128)} %get-tuple-element.259), channel_id=1, source_target_pairs={{0,16},{16,32},{32,48},{48,64},{64,80},{80,96},{96,112},{1,17},{17... | collective-permute-start | bytes 6152 | tf_op jit(solution)/shard_map/ppermute | solution.py:43
  99.1 4.8 %collective-permute-start.13 = (f32[2,256]{1,0:T(2,128)}, f32[2,256]{1,0:T(2,128)}, u32[]{:S(2)}, u32[]{:S(2)}) collective-permute-start(f32[2,256]{1,0:T(2,128)} %get-tuple-element.260), channel_id=1, source_target_pairs={{16,0},{32,16},{48,32},{64,48},{80,64},{96,80},{112,96},{17,1},{33... | collective-permute-start | bytes 6152 | tf_op jit(solution)/shard_map/ppermute | solution.py:46
  104.7 8.6 %collective-permute-start.14 = (f32[12,2]{1,0:T(8,128)S(1)}, f32[12,2]{1,0:T(8,128)S(1)}, u32[]{:S(2)}, u32[]{:S(2)}) collective-permute-start(f32[12,2]{1,0:T(8,128)S(1)} %get-tuple-element.250), channel_id=1, source_target_pairs={{0,1},{1,2},{2,3},{3,4},{4,5},{5,6},{6,7},{7,8},{8,9},{9,10},{10,1... | collective-permute-start | bytes 296 | tf_op jit(solution)/shard_map/ppermute | solution.py:43
  108.6 6.1 %collective-permute-start.15 = (f32[12,2]{1,0:T(8,128)S(1)}, f32[12,2]{1,0:T(8,128)S(1)}, u32[]{:S(2)}, u32[]{:S(2)}) collective-permute-start(f32[12,2]{1,0:T(8,128)S(1)} %get-tuple-element.251), channel_id=1, source_target_pairs={{1,0},{2,1},{3,2},{4,3},{5,4},{6,5},{7,6},{8,7},{9,8},{10,9},{11,1... | collective-permute-start | bytes 296 | tf_op jit(solution)/shard_map/ppermute | solution.py:46
  228.9 2.6 collective-permute-start.16
  230.2 3.1 collective-permute-start.17
  233.3 8.2 %collective-permute-start.18 = (f32[12,2]{1,0:T(8,128)S(1)}, f32[12,2]{1,0:T(8,128)S(1)}, u32[]{:S(2)}, u32[]{:S(2)}) collective-permute-start(f32[12,2]{1,0:T(8,128)S(1)} %get-tuple-element.248), channel_id=1, source_target_pairs={{0,1},{1,2},{2,3},{3,4},{4,5},{5,6},{6,7},{7,8},{8,9},{9,10},{10,1... | collective-permute-start | bytes 296 | tf_op jit(solution)/shard_map/ppermute | solution.py:43
  235.3 7.4 %collective-permute-start.19 = (f32[12,2]{1,0:T(8,128)S(1)}, f32[12,2]{1,0:T(8,128)S(1)}, u32[]{:S(2)}, u32[]{:S(2)}) collective-permute-start(f32[12,2]{1,0:T(8,128)S(1)} %get-tuple-element.249), channel_id=1, source_target_pairs={{1,0},{2,1},{3,2},{4,3},{5,4},{6,5},{7,6},{8,7},{9,8},{10,9},{11,1... | collective-permute-start | bytes 296 | tf_op jit(solution)/shard_map/ppermute | solution.py:46
  (62 other events, 392.6 us)
